TPU v7x, 32 devices: a whole 2x2x4 slice. The times are simulated.
32 devices in a mesh: grp: 2 (over y), ep: 4 (over x, core), hid: 4 (over z).
Axes of the slice: x: 2, y: 2, z: 4, core: 2. Of those that a mesh axis runs over, the one named last changes fastest.
Arguments:
- tokens: bfloat16 [1024, 4096], P(('grp', 'ep')), parts along dimension 0, may hold values from -6 to 6
- expert_ids: int32 [1024, 2], P(('grp', 'ep')), parts along dimension 0, may hold values from 0 to 3, all different within a row; in each aligned block of 128 rows (0 to 127, 128 to 255, ...) at most 64 rows name the same one
- gate_probs: float32 [1024, 2], P(('grp', 'ep')), parts along dimension 0, may hold values from 0.05 to 1
- w_gate: bfloat16 [16, 4096, 384], P(('ep', 'hid')), may hold values from -0.09375 to 0.09375
- w_up: bfloat16 [16, 4096, 384], P(('ep', 'hid')), may hold values from -0.09375 to 0.09375
- w_down: bfloat16 [16, 384, 4096], P(('ep', 'hid')), may hold values from -0.15625 to 0.15625
Outputs:
- mixed_out: bfloat16 [1024, 4096], P(('grp', 'ep'), 'hid'), parts along dimension 0
There are 2 independent parts, one for each index of `grp`. A program takes and returns all parts, laid end to end along the dimension named above; an argument that names none is the same for every part. Nothing has to cross between parts.
Inputs may be any that keep to these rules, and one draw needn't show every extreme that they name: `expert_ids`: each token names 2 different experts. Among the 128 tokens of one index of ep (aligned blocks of rows) no expert is named by more than 64 tokens, and in every draw some expert is named by exactly 64 tokens of some block.
All inputs are finite; a program needn't handle non-finite values.
Results may differ from a plain program's by a relative error of at most 0.0085.
Values may be sent and summed in bfloat16 or wider, within the bound.
A program may use at most 128 MiB of HBM per device.

v0:
```python
import jax
import jax.numpy as jnp
from jax import lax
from jax.sharding import PartitionSpec as P

QUARTERS = 4


def local(tokens, expert_ids, gate_probs, w_gate, w_up, w_down):
    ep_count = lax.axis_size("ep")
    hid_count = lax.axis_size("hid")
    tok_rows, model_width = tokens.shape
    pick_count = expert_ids.shape[1]
    groups = hid_count // QUARTERS
    experts = groups * ep_count
    capacity = tok_rows // 2
    hid_index = lax.axis_index("hid")
    group_index = hid_index // QUARTERS
    flat_ids = expert_ids.reshape(-1)
    onehot = (flat_ids[:, None] == jnp.arange(experts, dtype=jnp.int32)[None, :]).astype(jnp.int32)
    before = jnp.cumsum(onehot, axis=0) - onehot
    position = jnp.sum(before * onehot, axis=1)
    in_group = flat_ids % groups == group_index
    slot_index = jnp.where(in_group, flat_ids // groups * capacity + position, -1).reshape(
        tok_rows, pick_count
    )
    targets = jnp.arange(ep_count * capacity, dtype=jnp.int32)
    matches = slot_index[:, :, None] == targets[None, None, :]
    scatter_matrix = jnp.any(matches, axis=1).astype(jnp.bfloat16)
    gate_round = gate_probs.astype(jnp.bfloat16).astype(jnp.float32)
    combine_matrix = jnp.sum(jnp.where(matches, gate_round[:, :, None], 0.0), axis=1)
    outgoing = jnp.einsum("ts,td->sd", scatter_matrix, tokens, preferred_element_type=jnp.float32)
    outgoing = outgoing.astype(jnp.bfloat16).reshape(ep_count, capacity, model_width)
    gate_matrix = w_gate[0]
    up_matrix = w_up[0]
    down_matrix = w_down[0]
    slot_block = lax.all_to_all(outgoing, "ep", split_axis=0, concat_axis=0, tiled=True)
    gate_act = jnp.einsum(
        "scd,dh->sch", slot_block, gate_matrix, preferred_element_type=jnp.float32
    )
    up_act = jnp.einsum("scd,dh->sch", slot_block, up_matrix, preferred_element_type=jnp.float32)
    hidden = (jax.nn.silu(gate_act) * up_act).astype(jnp.bfloat16)
    partial_value = jnp.einsum(
        "sch,hd->scd", hidden, down_matrix, preferred_element_type=jnp.float32
    ).astype(jnp.bfloat16)
    returned = lax.all_to_all(partial_value, "ep", split_axis=0, concat_axis=0, tiled=True).reshape(
        ep_count * capacity, model_width
    )
    owner_term = jnp.dot(
        combine_matrix.astype(jnp.bfloat16), returned, preferred_element_type=jnp.float32
    )
    mixed_out = lax.psum_scatter(owner_term, "hid", scatter_dimension=1, tiled=True)
    return mixed_out.astype(jnp.bfloat16)


def solution(mesh):
    in_specs = (
        P(("grp", "ep"), None),
        P(("grp", "ep"), None),
        P(("grp", "ep"), None),
        P(("ep", "hid"), None, None),
        P(("ep", "hid"), None, None),
        P(("ep", "hid"), None, None),
    )
    out_specs = P(("grp", "ep"), "hid")
    return jax.shard_map(local, mesh=mesh, in_specs=in_specs, out_specs=out_specs, check_vma=False)
```

profile of v0, /device:TPU:0, one launch (start us, length us, event | category | flops | bytes accessed | tf_op | source)
XLA Modules:
  0.0 138.6 jit_solution(12919742394935414823)
XLA Ops:
  6.5 0.0 copy-start
  6.5 0.9 copy.25
  7.5 0.1 eq.54
  7.6 0.1 eq.50
  7.8 1.2 reduce-window.6
  9.0 0.1 slice.8
  9.1 0.1 copy.27
  9.2 0.1 copy.28
  9.3 0.1 add_bitcast_fusion
  9.4 0.1 reduce_sum.21
  9.6 0.1 copy.29
  9.6 0.7 add_select_fusion
  10.3 0.1 fusion.18
  10.5 2.0 %convolution_convert_fusion = bf16[256,4096]{1,0:T(8,128)(2,1)S(1)} fusion(pred[128,256]{1,0:T(8,128)(4,1)S(1)} %fusion.18, bf16[128,4096]{1,0:T(8,128)(2,1)} %param.6), kind=kOutput, calls=%fused_computation | convolution fusion | flops 269484032 | bytes 3178496 | tf_op jit(solution)/shard_map/ts,td->sd/dot_general | solution.py:32
  12.4 0.0 copy-start.3
  12.4 30.0 %all_to_all.10 = bf16[4,64,4096]{2,1,0:T(8,128)(2,1)S(1)} all-to-all(bf16[4,64,4096]{2,1,0:T(8,128)(2,1)S(1)} %bitcast.45), channel_id=1, replica_groups=mesh['grp'=2,'ep'=4,'hid'=4] {'ep'}, dimensions={0} | all-to-all | bytes 4194304 | tf_op jit(solution)/shard_map/all_to_all | solution.py:37
  42.4 0.0 copy-start.1
  42.4 1.3 copy-done.1
  43.7 0.0 copy-done.3
  43.7 2.1 %fusion.3 = f32[4,64,384]{2,1,0:T(8,128)} fusion(bf16[4,64,4096]{2,1,0:T(8,128)(2,1)S(1)} %all_to_all.10, bf16[1,4096,384]{2,1,0:T(8,128)(2,1)S(1)} %copy-done.3), kind=kOutput, calls=%fused_computation.5 | convolution fusion | flops 805306368 | bytes 5636096 | tf_op jit(solution)/shard_map/scd,dh->sch/dot_general | solution.py:38
  45.8 0.0 copy-done
  45.8 6.4 %convolution_convert_fusion.1 = bf16[4,64,4096]{2,1,0:T(8,128)(2,1)} fusion(bf16[1,384,4096]{2,1,0:T(8,128)(2,1)S(1)} %copy-done, bf16[4,64,4096]{2,1,0:T(8,128)(2,1)} %copy-done.1, bf16[1,4096,384]{2,1,0:T(8,128)(2,1)} %param.10, f32[4,64,384]{2,1,0:T(8,128)} %fusion.3), kind=kOutput, calls=%fused_computation.1 | convolution fusion | flops 1612251136 | bytes 10878976 | tf_op jit(solution)/shard_map/sch,hd->scd/dot_general | solution.py:43
  52.1 0.0 copy-start.2
  52.1 4.6 %all-to-all-start.1 = ((bf16[4,64,4096]{2,1,0:T(8,128)(2,1)}), bf16[4,64,4096]{2,1,0:T(8,128)(2,1)}, u32[]{:S(2)}, u32[]{:S(2)}) async-start(bf16[4,64,4096]{2,1,0:T(8,128)(2,1)} %convolution_convert_fusion.1), calls=%async_computation.1 | async-start | bytes 4194304 | tf_op jit(solution)/shard_map/all_to_all | solution.py:46
  56.7 0.0 reduce-scatter.2.cloned.1.call-start
  56.8 0.0 copy-done.2
  56.8 0.1 select_reduce_fusion
  56.9 25.5 %all-to-all-done.1 = bf16[4,64,4096]{2,1,0:T(8,128)(2,1)} async-done(((bf16[4,64,4096]{2,1,0:T(8,128)(2,1)}), bf16[4,64,4096]{2,1,0:T(8,128)(2,1)}, u32[]{:S(2)}, u32[]{:S(2)}) %all-to-all-start.1) | async-done | bytes 2097184 | tf_op jit(solution)/shard_map/all_to_all | solution.py:46
  82.5 3.4 %fusion.26 = f32[128,4096]{1,0:T(8,128)} fusion(bf16[128,256]{1,0:T(8,128)(2,1)S(1)} %select_reduce_fusion, bf16[256,4096]{1,0:T(8,128)(2,1)} %bitcast.9), kind=kOutput, calls=%fused_computation.30 | convolution fusion | flops 268435456 | bytes 4259840 | tf_op jit(solution)/shard_map/dot_general | solution.py:49
  85.8 0.0 reduce-scatter.2.cloned.1.call-update
  85.9 44.1 %reduce-scatter.2.cloned.1.call-done = f32[128,1024]{1,0:T(8,128)} async-done(((f32[128,4096]{1,0:T(8,128)}), f32[128,1024]{1,0:T(8,128)}) %reduce-scatter.2.cloned.1.call-update) | async-done | bytes 524304 | tf_op jit(solution)/shard_map/reduce_scatter | solution.py:52
  130.0 1.8 %convert_element_type.37 = bf16[128,1024]{1,0:T(8,128)(2,1)} convert(f32[128,1024]{1,0:T(8,128)} %reduce-scatter.2.cloned.1.call-done) | non-fusion elementwise | flops 131072 | bytes 786432 | tf_op jit(solution)/shard_map/convert_element_type | solution.py:53
  (5 shorter events, 0.1 us)
Async XLA Ops:
  6.5 39.2 %copy-start = (bf16[1,384,4096]{2,1,0:T(8,128)(2,1)S(1)}, bf16[1,384,4096]{2,1,0:T(8,128)(2,1)}, u32[]{:S(2)}) copy-start(bf16[1,384,4096]{2,1,0:T(8,128)(2,1)} %param.11) | copy-start | bytes 9437188
  12.4 31.3 %copy-start.3 = (bf16[1,4096,384]{2,1,0:T(8,128)(2,1)S(1)}, bf16[1,4096,384]{2,1,0:T(8,128)(2,1)}, u32[]{:S(2)}) copy-start(bf16[1,4096,384]{2,1,0:T(8,128)(2,1)} %param.9) | copy-start | bytes 9437188
  42.4 1.3 copy-start.1
  52.1 4.6 %copy-start.2 = (f32[128,2]{0,1:T(2,128)S(1)}, f32[128,2]{0,1:T(2,128)}, u32[]{:S(2)}) copy-start(f32[128,2]{0,1:T(2,128)} %param.8) | copy-start | bytes 3076
  52.1 30.3 %all-to-all-start.1 = ((bf16[4,64,4096]{2,1,0:T(8,128)(2,1)}), bf16[4,64,4096]{2,1,0:T(8,128)(2,1)}, u32[]{:S(2)}, u32[]{:S(2)}) async-start(bf16[4,64,4096]{2,1,0:T(8,128)(2,1)} %convolution_convert_fusion.1), calls=%async_computation.1 | async-start | bytes 4194304 | tf_op jit(solution)/shard_map/all_to_all | solution.py:46
  56.7 73.2 %reduce-scatter.2.cloned.1.call-start = ((), (), s32[]{:S(2)}) async-start(), calls=%async_computation.3 | async-start | bytes 2621440 | tf_op jit(solution)/shard_map/reduce_scatter | solution.py:52
Sparse Core Ops, SparseCore 0:
  86.0 43.9 reduce-scatter.1
where the time goes:
time: 139 us
  waiting for transfers between devices  69.6 us (50%)
  blocking collectives  30 us (22%)
  matrix products  13.8 us (10%)
  between operations  13.5 us (10%)
  starting transfers between devices  4.62 us (3%)
  other arithmetic  4.09 us (3%)
  local copies, waits for them, and re-layouts  2.99 us (2%)
    reduce_scatter x1, waiting for transfers between devices, local(): lax.psum_scatter(owner_term, 'hid', scatter_dimension=1, tiled=True)  44.1 us
    all_to_all x1, blocking collectives, local(): lax.all_to_all(outgoing, 'ep', split_axis=0, concat_axis=0, tiled=True)  30 us
    all_to_all x1, waiting for transfers between devices, local(): lax.all_to_all(partial_value, 'ep', split_axis=0, concat_axis=0, tiled=True)  25.5 us
    dot_general x1, matrix products, local(): jnp.einsum('sch,hd->scd', hidden, down_matrix, preferred_element_type=jnp...  6.37 us
    all_to_all x1, starting transfers between devices, local(): lax.all_to_all(partial_value, 'ep', split_axis=0, concat_axis=0, tiled=True)  4.58 us
    dot_general x1, matrix products, local(): jnp.dot(combine_matrix.astype(jnp.bfloat16), returned, preferred_element_...  3.39 us
  transfers between devices with their start and end apart: 2, of which 2 were waited for; matrix products, arithmetic and copies ran while one was open for 0% of the time, Pallas kernels for 0%

commit v1 on v0

v1 whole, which is shorter than its diff:
```python
import functools

import jax
import jax.numpy as jnp
from jax import lax
from jax.experimental import pallas as pl
from jax.experimental.pallas import tpu as pltpu
from jax.sharding import PartitionSpec as P

QUARTERS = 4
ROW_CHUNKS = 2
RETURN_CHUNKS = 4
MESH = pl.DeviceIdType.MESH
F32 = jnp.float32
BF16 = jnp.bfloat16


def kernel(ep_count, hid_count, tokens, ids, probs, w_gate, w_up, w_down, out,
           gate_buf, up_buf, down_buf, key_t, combine, outgoing, sibling_out, slots, hidden,
           partial, returned, owner_out, owner_in,
           weight_sem, disp_send, disp_recv, fwd_send, fwd_recv, ret_send, ret_recv, sum_send, sum_recv):
    ep = lax.axis_index("ep")
    hid = lax.axis_index("hid")
    groups = hid_count // QUARTERS
    group = hid // QUARTERS
    rows, width = tokens.shape
    picks = ids.shape[1]
    cap = slots.shape[1]
    half = width // 2
    pairs = ep_count // 2
    pair = ep // 2
    core = ep % 2
    sibling = pair * 2 + 1 - core
    mate = hid + 1 - 2 * (hid % 2)
    my_half = pl.ds(pl.multiple_of((hid % 2) * half, half), half)
    piece = cap // ROW_CHUNKS
    feat = width // hid_count
    chunks = partial.shape[0]
    step = feat // chunks

    loads = [pltpu.make_async_copy(src.at[0], dst, weight_sem.at[i])
             for i, (src, dst) in enumerate(((w_gate, gate_buf), (w_up, up_buf), (w_down, down_buf)))]
    for load in loads:
        load.start()

    barrier = pltpu.get_barrier_semaphore()
    for off in range(1, ep_count):
        pl.semaphore_signal(barrier, 1, device_id={"ep": lax.rem(ep + off, ep_count)}, device_id_type=MESH)
    for off in range(1, hid_count):
        pl.semaphore_signal(barrier, 1, device_id={"hid": lax.rem(hid + off, hid_count)}, device_id_type=MESH)

    lane = lax.broadcasted_iota(jnp.int32, (rows, 128), 1) * groups + group
    count = jnp.zeros((rows, 128), F32)
    weight = jnp.zeros((rows, 128), F32)
    gate_round = probs[...].astype(BF16).astype(F32)
    for k in range(picks):
        hit = ids[:, k:k + 1] == lane
        count = jnp.where(hit, 1.0, count)
        weight = jnp.where(hit, gate_round[:, k:k + 1], weight)
    earlier = (lax.broadcasted_iota(jnp.int32, (rows, rows), 1)
               < lax.broadcasted_iota(jnp.int32, (rows, rows), 0)).astype(F32).astype(BF16)
    before = jnp.dot(earlier, count.astype(BF16), preferred_element_type=F32)
    key = jnp.where(count > 0.5, before, -1000.0).astype(jnp.int32)
    key_t[...] = jnp.where(count > 0.5, before, -1000.0).T.astype(jnp.int32)

    def pick_rows(first, blocks):
        row = lax.broadcasted_iota(jnp.int32, (cap, rows), 0)
        parts = [(key_t[pl.ds(first + b, 1), :] == row).astype(F32).astype(BF16) for b in range(blocks)]
        return jnp.concatenate(parts, axis=0) if blocks > 1 else parts[0]

    tile = min(half, 512)
    sends = []
    for off in range(1, pairs):
        other = lax.rem(pair + off, pairs)
        chosen = pick_rows(2 * other, 2)
        for col in range(0, half, tile):
            src = pl.ds(pl.multiple_of((hid % 2) * half + col, tile), tile)
            rows_out = jnp.dot(chosen, tokens[:, src], preferred_element_type=F32).astype(BF16)
            outgoing[off - 1, :, :, col:col + tile] = rows_out.reshape(2, cap, tile)
    pl.semaphore_wait(barrier, ep_count - 1 + hid_count - 1)
    for off in range(1, pairs):
        other = lax.rem(pair + off, pairs)
        for r in range(ROW_CHUNKS):
            part = pl.ds(r * piece, piece)
            for flip in range(2):
                who = core if flip == 0 else 1 - core
                copy = pltpu.make_async_remote_copy(
                    src_ref=outgoing.at[off - 1, who, part],
                    dst_ref=slots.at[ep, part, my_half],
                    send_sem=disp_send.at[off, r, flip],
                    recv_sem=disp_recv.at[ep, r],
                    device_id={"ep": 2 * other + who}, device_id_type=MESH)
                copy.start()
                sends.append(copy)

    for col in range(0, width, tile):
        sibling_out[:, col:col + tile] = jnp.dot(
            pick_rows(sibling, 1), tokens[:, col:col + tile], preferred_element_type=F32).astype(BF16)
    to_sibling = pltpu.make_async_remote_copy(
        src_ref=sibling_out, dst_ref=slots.at[ep],
        send_sem=disp_send.at[0, 0, 0], recv_sem=disp_recv.at[ep, 0],
        device_id={"ep": sibling}, device_id_type=MESH)
    to_sibling.start()
    sends.append(to_sibling)
    for col in range(0, width, tile):
        slots[ep, :, col:col + tile] = jnp.dot(
            pick_rows(ep, 1), tokens[:, col:col + tile], preferred_element_type=F32).astype(BF16)

    lanes = lax.broadcasted_iota(jnp.int32, (rows, cap), 1)
    for b in range(ep_count):
        combine[:, b * cap:(b + 1) * cap] = jnp.where(
            key[:, b:b + 1] == lanes, weight[:, b:b + 1], 0.0).astype(BF16)

    def act(which):
        block = slots[pl.ds(2 * which, 2)].reshape(2 * cap, width)
        gate_act = jnp.dot(block, gate_buf[...], preferred_element_type=F32)
        up_act = jnp.dot(block, up_buf[...], preferred_element_type=F32)
        value = gate_act / (1.0 + jnp.exp(-gate_act)) * up_act
        hidden[pl.ds(pl.multiple_of(which * 2 * cap, 2 * cap), 2 * cap), :] = value.astype(BF16)

    pltpu.make_async_remote_copy(
        src_ref=sibling_out, dst_ref=slots.at[sibling],
        send_sem=disp_send.at[0, 0, 0], recv_sem=disp_recv.at[sibling, 0],
        device_id={"ep": sibling}, device_id_type=MESH).wait_recv()
    loads[0].wait()
    loads[1].wait()
    act(pair)

    forwards = []
    for off in range(1, pairs):
        other = lax.rem(pair + pairs - off, pairs)
        for r in range(ROW_CHUNKS):
            part = pl.ds(r * piece, piece)
            for flip in range(2):
                source = 2 * other + (core if flip == 0 else 1 - core)
                landed = slots.at[source, part, my_half]
                pltpu.make_async_remote_copy(
                    src_ref=landed, dst_ref=landed,
                    send_sem=disp_send.at[off, r, flip], recv_sem=disp_recv.at[source, r],
                    device_id={"ep": source}, device_id_type=MESH).wait_recv()
                copy = pltpu.make_async_remote_copy(
                    src_ref=landed, dst_ref=landed,
                    send_sem=fwd_send.at[off, r, flip], recv_sem=fwd_recv.at[off, r, flip],
                    device_id={"hid": mate}, device_id_type=MESH)
                copy.start()
                forwards.append(copy)
    per = 2 * ROW_CHUNKS
    for off in range(1, pairs):
        for copy in forwards[(off - 1) * per:off * per]:
            copy.wait_recv()
        act(lax.rem(pair + pairs - off, pairs))

    loads[2].wait()
    for c in range(chunks):
        for h in range(hid_count):
            col = h * feat + c * step
            value = jnp.dot(hidden[...], down_buf[:, col:col + step], preferred_element_type=F32)
            partial[c, :, :, h * step:(h + 1) * step] = value.astype(BF16).reshape(ep_count, cap, step)
        for off in list(range(2, ep_count)) + [1]:
            owner = lax.rem(ep + off, ep_count)
            copy = pltpu.make_async_remote_copy(
                src_ref=partial.at[c, owner], dst_ref=returned.at[c, ep],
                send_sem=ret_send.at[c, off], recv_sem=ret_recv.at[c, ep],
                device_id={"ep": owner}, device_id_type=MESH)
            copy.start()
            sends.append(copy)
        returned[c, ep] = partial[c, ep]

    for c in range(chunks):
        for off in range(1, ep_count):
            source = lax.rem(ep + off, ep_count)
            pltpu.make_async_remote_copy(
                src_ref=partial.at[c, source], dst_ref=returned.at[c, source],
                send_sem=ret_send.at[c, off], recv_sem=ret_recv.at[c, source],
                device_id={"ep": source}, device_id_type=MESH).wait_recv()
        for h in range(hid_count):
            block = returned[c, :, :, h * step:(h + 1) * step].reshape(ep_count * cap, step)
            owner_out[c, h] = jnp.dot(combine[...], block, preferred_element_type=F32).astype(BF16)
        for off in list(range(2, hid_count)) + [1]:
            target = lax.rem(hid + off, hid_count)
            copy = pltpu.make_async_remote_copy(
                src_ref=owner_out.at[c, target], dst_ref=owner_in.at[c, hid],
                send_sem=sum_send.at[c, off], recv_sem=sum_recv.at[c, hid],
                device_id={"hid": target}, device_id_type=MESH)
            copy.start()
            sends.append(copy)

    for c in range(chunks):
        total = owner_out[c, hid].astype(F32)
        for off in range(1, hid_count):
            source = lax.rem(hid + off, hid_count)
            pltpu.make_async_remote_copy(
                src_ref=owner_out.at[c, source], dst_ref=owner_in.at[c, source],
                send_sem=sum_send.at[c, off], recv_sem=sum_recv.at[c, source],
                device_id={"hid": source}, device_id_type=MESH).wait_recv()
            total = total + owner_in[c, source].astype(F32)
        out[:, c * step:(c + 1) * step] = total.astype(BF16)
    for copy in sends + forwards:
        copy.wait_send()


def local(ep_count, hid_count, tokens, expert_ids, gate_probs, w_gate, w_up, w_down):
    rows, width = tokens.shape
    inner = w_gate.shape[2]
    cap = rows // 2
    feat = width // hid_count
    chunks = RETURN_CHUNKS
    step = feat // chunks
    others = max(ep_count // 2 - 1, 1)
    vmem = pl.BlockSpec(memory_space=pltpu.VMEM)
    hbm = pl.BlockSpec(memory_space=pl.ANY)
    dma = pltpu.SemaphoreType.DMA
    return pl.pallas_call(
        functools.partial(kernel, ep_count, hid_count),
        out_shape=jax.ShapeDtypeStruct((rows, feat), BF16),
        in_specs=[vmem, vmem, vmem, hbm, hbm, hbm],
        out_specs=vmem,
        scratch_shapes=[
            pltpu.VMEM((width, inner), BF16),
            pltpu.VMEM((width, inner), BF16),
            pltpu.VMEM((inner, width), BF16),
            pltpu.VMEM((128, rows), jnp.int32),
            pltpu.VMEM((rows, ep_count * cap), BF16),
            pltpu.VMEM((others, 2, cap, width // 2), BF16),
            pltpu.VMEM((cap, width), BF16),
            pltpu.VMEM((ep_count, cap, width), BF16),
            pltpu.VMEM((ep_count * cap, inner), BF16),
            pltpu.VMEM((chunks, ep_count, cap, hid_count * step), BF16),
            pltpu.VMEM((chunks, ep_count, cap, hid_count * step), BF16),
            pltpu.VMEM((chunks, hid_count, rows, step), BF16),
            pltpu.VMEM((chunks, hid_count, rows, step), BF16),
            dma((3,)),
            dma((ep_count // 2, ROW_CHUNKS, 2)),
            dma((ep_count, ROW_CHUNKS)),
            dma((ep_count // 2, ROW_CHUNKS, 2)),
            dma((ep_count // 2, ROW_CHUNKS, 2)),
            dma((chunks, ep_count)),
            dma((chunks, ep_count)),
            dma((chunks, hid_count)),
            dma((chunks, hid_count)),
        ],
        compiler_params=pltpu.CompilerParams(
            collective_id=0, has_side_effects=True, vmem_limit_bytes=60 * 2**20),
    )(tokens, expert_ids, gate_probs, w_gate, w_up, w_down)


def solution(mesh):
    in_specs = (
        P(("grp", "ep"), None),
        P(("grp", "ep"), None),
        P(("grp", "ep"), None),
        P(("ep", "hid"), None, None),
        P(("ep", "hid"), None, None),
        P(("ep", "hid"), None, None),
    )
    out_specs = P(("grp", "ep"), "hid")
    body = functools.partial(local, mesh.shape["ep"], mesh.shape["hid"])
    return jax.shard_map(body, mesh=mesh, in_specs=in_specs, out_specs=out_specs, check_vma=False)
```

time: 139 us -> 62.5 us (0.45)
  waiting for transfers between devices: 69.6 us -> 0 us
  Pallas kernels: 0 us -> 57.9 us
  blocking collectives: 30 us -> 0 us
  matrix products: 13.8 us -> 0 us
  between operations: 13.5 us -> 0.01 us
  starting transfers between devices: 4.62 us -> 0 us
  other arithmetic: 4.09 us -> 0 us
  local copies, waits for them, and re-layouts: 2.99 us -> 4.48 us
    pallas_call x0 -> x1, Pallas kernels: none -> 57.9 us  [local(): pl.pallas_call(functools.partial(kernel, ep_count, hid_count), out_shape=...]
    reduce_scatter x1 -> x0, waiting for transfers between devices: 44.1 us -> none  [local(): lax.psum_scatter(owner_term, 'hid', scatter_dimension=1, tiled=True)]
    all_to_all x1 -> x0, blocking collectives: 30 us -> none  [local(): lax.all_to_all(outgoing, 'ep', split_axis=0, concat_axis=0, tiled=True)]
    all_to_all x1 -> x0, waiting for transfers between devices: 25.5 us -> none  [local(): lax.all_to_all(partial_value, 'ep', split_axis=0, concat_axis=0, tiled=True)]
    dot_general x4 -> x0, matrix products: 13.8 us -> none  [the longest x1 6.37 us: local(): jnp.einsum('sch,hd->scd', hidden, down_matrix, preferred_element_type=jnp...]
    all_to_all x1 -> x0, starting transfers between devices: 4.58 us -> none  [local(): lax.all_to_all(partial_value, 'ep', split_axis=0, concat_axis=0, tiled=True)]
    unnamed x9 -> x3, local copies, waits for them, and re-layouts: 2.24 us -> 4.48 us
    convert_element_type x3 -> x0, other arithmetic: 1.78 us -> none  [the longest x1 1.78 us: local(): return mixed_out.astype(jnp.bfloat16)]
  transfers between devices with their start and end apart: 2 -> 0, of which waited for: 2 -> 0; matrix products, arithmetic and copies ran while one was open for 0% -> 0% of each run, Pallas kernels for 0% -> 0%
where the time goes in v1:
time: 62.5 us; the launch traced here: 62.3 us
  Pallas kernels  57.9 us (93%)
  local copies, waits for them, and re-layouts  4.48 us (7%)
    pallas_call x1, Pallas kernels, local(): pl.pallas_call(functools.partial(kernel, ep_count, hid_count), out_shape=...  57.9 us
    unnamed x3, local copies, waits for them, and re-layouts  4.48 us

profile of v1, /device:TPU:0, one launch (start us, length us, event | category | flops | bytes accessed | tf_op | source)
XLA Modules:
  0.0 62.3 jit_solution(961833365942036169)
XLA Ops:
  0.0 1.4 %copy.7.ids = s32[128,2]{1,0:T(8,128)} copy(s32[128,2]{0,1:T(2,128)} %param.7) | data formatting | bytes 2048 | tf_op args[1]
  1.4 1.4 %copy.8.probs = f32[128,2]{1,0:T(8,128)} copy(f32[128,2]{0,1:T(2,128)} %param.8) | data formatting | bytes 2048 | tf_op args[2]
  2.8 57.9 %shard_map.64 = bf16[128,1024]{1,0:T(8,128)(2,1)} custom-call(bf16[128,4096]{1,0:T(8,128)(2,1)} %tokens.1, s32[128,2]{1,0:T(8,128)} %copy.7.ids, f32[128,2]{1,0:T(8,128)} %copy.8.probs, bf16[1,4096,384]{2,1,0:T(8,128)(2,1)} %w_gate.1, bf16[1,4096,384]{2,1,0:T(8,128)(2,1)} %w_up.1, bf16[1,384,4096]{2,1,0:T(8,128)(2,1)} %w_down.1), custom_call_target="tpu_custom_call" | custom-call | tf_op jit(solution)/shard_map/pallas_call | solution.py:213
  60.7 1.7 %copy.10 = bf16[128,1024]{1,0:T(8,128)(2,1)} copy(bf16[128,1024]{1,0:T(8,128)(2,1)} %shard_map.64) | data formatting | bytes 524288

commit v2 on v1

--- a/solution.py
+++ b/solution.py
@@ -8,8 +8,8 @@
 from jax.sharding import PartitionSpec as P
 
 QUARTERS = 4
-ROW_CHUNKS = 2
-RETURN_CHUNKS = 4
+ROW_CHUNKS = 4
+RETURN_STEP = 128
 MESH = pl.DeviceIdType.MESH
 F32 = jnp.float32
 BF16 = jnp.bfloat16
@@ -24,7 +24,7 @@
     groups = hid_count // QUARTERS
     group = hid // QUARTERS
     rows, width = tokens.shape
-    picks = ids.shape[1]
+    picks = ids.shape[0]
     cap = slots.shape[1]
     half = width // 2
     pairs = ep_count // 2
@@ -49,19 +49,19 @@
     for off in range(1, hid_count):
         pl.semaphore_signal(barrier, 1, device_id={"hid": lax.rem(hid + off, hid_count)}, device_id_type=MESH)
 
-    lane = lax.broadcasted_iota(jnp.int32, (rows, 128), 1) * groups + group
-    count = jnp.zeros((rows, 128), F32)
-    weight = jnp.zeros((rows, 128), F32)
+    name = lax.broadcasted_iota(jnp.int32, (128, rows), 0) * groups + group
+    count = jnp.zeros((128, rows), F32)
+    weight = jnp.zeros((128, rows), F32)
     gate_round = probs[...].astype(BF16).astype(F32)
     for k in range(picks):
-        hit = ids[:, k:k + 1] == lane
+        hit = ids[k:k + 1, :] == name
         count = jnp.where(hit, 1.0, count)
-        weight = jnp.where(hit, gate_round[:, k:k + 1], weight)
-    earlier = (lax.broadcasted_iota(jnp.int32, (rows, rows), 1)
-               < lax.broadcasted_iota(jnp.int32, (rows, rows), 0)).astype(F32).astype(BF16)
-    before = jnp.dot(earlier, count.astype(BF16), preferred_element_type=F32)
-    key = jnp.where(count > 0.5, before, -1000.0).astype(jnp.int32)
-    key_t[...] = jnp.where(count > 0.5, before, -1000.0).T.astype(jnp.int32)
+        weight = jnp.where(hit, gate_round[k:k + 1, :], weight)
+    earlier = (lax.broadcasted_iota(jnp.int32, (rows, rows), 0)
+               < lax.broadcasted_iota(jnp.int32, (rows, rows), 1)).astype(F32).astype(BF16)
+    before = jnp.dot(count.astype(BF16), earlier, preferred_element_type=F32)
+    place = jnp.where(count > 0.5, before, -1000.0)
+    key_t[...] = place.astype(jnp.int32)
 
     def pick_rows(first, blocks):
         row = lax.broadcasted_iota(jnp.int32, (cap, rows), 0)
@@ -107,6 +107,8 @@
             pick_rows(ep, 1), tokens[:, col:col + tile], preferred_element_type=F32).astype(BF16)
 
     lanes = lax.broadcasted_iota(jnp.int32, (rows, cap), 1)
+    key = place.T.astype(jnp.int32)
+    weight = weight.T
     for b in range(ep_count):
         combine[:, b * cap:(b + 1) * cap] = jnp.where(
             key[:, b:b + 1] == lanes, weight[:, b:b + 1], 0.0).astype(BF16)
@@ -204,8 +206,8 @@
     inner = w_gate.shape[2]
     cap = rows // 2
     feat = width // hid_count
-    chunks = RETURN_CHUNKS
-    step = feat // chunks
+    step = RETURN_STEP
+    chunks = feat // step
     others = max(ep_count // 2 - 1, 1)
     vmem = pl.BlockSpec(memory_space=pltpu.VMEM)
     hbm = pl.BlockSpec(memory_space=pl.ANY)
@@ -241,7 +243,7 @@
         ],
         compiler_params=pltpu.CompilerParams(
             collective_id=0, has_side_effects=True, vmem_limit_bytes=60 * 2**20),
-    )(tokens, expert_ids, gate_probs, w_gate, w_up, w_down)
+    )(tokens, expert_ids.T, gate_probs.T, w_gate, w_up, w_down)
 
 
 def solution(mesh):

time: 62.5 us -> 57.6 us (0.922)
  local copies, waits for them, and re-layouts: 4.48 us -> 1.67 us
  Pallas kernels: 57.9 us -> 55.7 us
    unnamed x3 -> x1, local copies, waits for them, and re-layouts: 4.48 us -> 1.67 us
    pallas_call x1, Pallas kernels: 57.9 us -> 55.7 us  [local(): pl.pallas_call(functools.partial(kernel, ep_count, hid_count), out_shape=...]
where the time goes in v2:
time: 57.6 us; the launch traced here: 57.4 us
  Pallas kernels  55.7 us (97%)
  local copies, waits for them, and re-layouts  1.67 us (3%)
    pallas_call x1, Pallas kernels, local(): pl.pallas_call(functools.partial(kernel, ep_count, hid_count), out_shape=...  55.7 us
    unnamed x1, local copies, waits for them, and re-layouts  1.67 us

profile of v2, /device:TPU:0, one launch (start us, length us, event | category | flops | bytes accessed | tf_op | source)
XLA Modules:
  0.0 57.4 jit_solution(11646693916112906472)
XLA Ops:
  0.0 55.7 %shard_map.64 = bf16[128,1024]{1,0:T(8,128)(2,1)} custom-call(bf16[128,4096]{1,0:T(8,128)(2,1)} %tokens.1, s32[2,128]{1,0:T(2,128)} %bitcast.2, f32[2,128]{1,0:T(2,128)} %bitcast.3, bf16[1,4096,384]{2,1,0:T(8,128)(2,1)} %w_gate.1, bf16[1,4096,384]{2,1,0:T(8,128)(2,1)} %w_up.1, bf16[1,384,4096]{2,1,0:T(8,128)(2,1)} %w_down.1), custom_call_target="tpu_custom_call" | custom-call | tf_op jit(solution)/shard_map/pallas_call | solution.py:215
  55.7 1.7 %copy.8 = bf16[128,1024]{1,0:T(8,128)(2,1)} copy(bf16[128,1024]{1,0:T(8,128)(2,1)} %shard_map.64) | data formatting | bytes 524288

commit v3 on v2

--- a/solution.py
+++ b/solution.py
@@ -36,6 +36,8 @@
     piece = cap // ROW_CHUNKS
     feat = width // hid_count
     chunks = partial.shape[0]
+    inner = gate_buf.shape[1]
+    row_groups = ((0, 1), (1, ROW_CHUNKS)) if pairs == 2 else ((0, ROW_CHUNKS),)
     step = feat // chunks
 
     loads = [pltpu.make_async_copy(src.at[0], dst, weight_sem.at[i])
@@ -113,12 +115,35 @@
         combine[:, b * cap:(b + 1) * cap] = jnp.where(
             key[:, b:b + 1] == lanes, weight[:, b:b + 1], 0.0).astype(BF16)
 
-    def act(which):
-        block = slots[pl.ds(2 * which, 2)].reshape(2 * cap, width)
+    def act(which, start, size):
+        block = slots[pl.ds(2 * which, 2), start:start + size].reshape(2 * size, width)
         gate_act = jnp.dot(block, gate_buf[...], preferred_element_type=F32)
         up_act = jnp.dot(block, up_buf[...], preferred_element_type=F32)
         value = gate_act / (1.0 + jnp.exp(-gate_act)) * up_act
-        hidden[pl.ds(pl.multiple_of(which * 2 * cap, 2 * cap), 2 * cap), :] = value.astype(BF16)
+        hidden[pl.ds(2 * which, 2), start:start + size] = value.astype(BF16).reshape(2, size, inner)
+
+    def down(first, pair_count, start, size, c):
+        block = hidden[pl.ds(2 * first, 2 * pair_count), start:start + size]
+        block = block.reshape(2 * pair_count * size, inner)
+        for h in range(hid_count):
+            col = h * feat + c * step
+            value = jnp.dot(block, down_buf[:, col:col + step], preferred_element_type=F32)
+            partial[c, pl.ds(2 * first, 2 * pair_count), start:start + size, h * step:(h + 1) * step] = (
+                value.astype(BF16).reshape(2 * pair_count, size, step))
+
+    def give_back(owner, start, size, c, g):
+        return pltpu.make_async_remote_copy(
+            src_ref=partial.at[c, owner, pl.ds(start, size)],
+            dst_ref=returned.at[c, ep, pl.ds(start, size)],
+            send_sem=ret_send.at[c, owner, g], recv_sem=ret_recv.at[c, ep, g],
+            device_id={"ep": owner}, device_id_type=MESH)
+
+    def take_back(source, start, size, c, g):
+        landed = returned.at[c, source, pl.ds(start, size)]
+        pltpu.make_async_remote_copy(
+            src_ref=landed, dst_ref=landed,
+            send_sem=ret_send.at[c, source, g], recv_sem=ret_recv.at[c, source, g],
+            device_id={"ep": source}, device_id_type=MESH).wait_recv()
 
     pltpu.make_async_remote_copy(
         src_ref=sibling_out, dst_ref=slots.at[sibling],
@@ -126,13 +151,14 @@
         device_id={"ep": sibling}, device_id_type=MESH).wait_recv()
     loads[0].wait()
     loads[1].wait()
-    act(pair)
-
-    forwards = []
-    for off in range(1, pairs):
-        other = lax.rem(pair + pairs - off, pairs)
-        for r in range(ROW_CHUNKS):
-            part = pl.ds(r * piece, piece)
+    act(pair, 0, cap)
+
+    forwards = {}
+
+    def forward(r):
+        part = pl.ds(r * piece, piece)
+        for off in range(1, pairs):
+            other = lax.rem(pair + pairs - off, pairs)
             for flip in range(2):
                 source = 2 * other + (core if flip == 0 else 1 - core)
                 landed = slots.at[source, part, my_half]
@@ -145,36 +171,47 @@
                     send_sem=fwd_send.at[off, r, flip], recv_sem=fwd_recv.at[off, r, flip],
                     device_id={"hid": mate}, device_id_type=MESH)
                 copy.start()
-                forwards.append(copy)
-    per = 2 * ROW_CHUNKS
-    for off in range(1, pairs):
-        for copy in forwards[(off - 1) * per:off * per]:
-            copy.wait_recv()
-        act(lax.rem(pair + pairs - off, pairs))
+                forwards[off, r, flip] = copy
 
     loads[2].wait()
+    passed = 0
+    for g, (low, high) in enumerate(row_groups):
+        start, size = low * piece, (high - low) * piece
+        last = g == len(row_groups) - 1
+        for r in range(passed, ROW_CHUNKS if last else high + 1):
+            forward(r)
+        passed = high + 1
+        for off in range(1, pairs):
+            for r in range(low, high):
+                for flip in range(2):
+                    forwards[off, r, flip].wait_recv()
+            act(lax.rem(pair + pairs - off, pairs), start, size)
+        for c in range(chunks):
+            if len(row_groups) > 1:
+                down(1 - pair, 1, start, size, c)
+            else:
+                down(0, pairs, 0, cap, c)
+            for off in range(1, pairs):
+                other = lax.rem(pair + off, pairs)
+                for who in (core, 1 - core):
+                    copy = give_back(2 * other + who, start, size, c, g)
+                    copy.start()
+                    sends.append(copy)
+            if last:
+                if len(row_groups) > 1:
+                    down(pair, 1, 0, cap, c)
+                copy = give_back(sibling, 0, cap, c, 0)
+                copy.start()
+                sends.append(copy)
+                returned[c, ep] = partial[c, ep]
+
     for c in range(chunks):
-        for h in range(hid_count):
-            col = h * feat + c * step
-            value = jnp.dot(hidden[...], down_buf[:, col:col + step], preferred_element_type=F32)
-            partial[c, :, :, h * step:(h + 1) * step] = value.astype(BF16).reshape(ep_count, cap, step)
-        for off in list(range(2, ep_count)) + [1]:
-            owner = lax.rem(ep + off, ep_count)
-            copy = pltpu.make_async_remote_copy(
-                src_ref=partial.at[c, owner], dst_ref=returned.at[c, ep],
-                send_sem=ret_send.at[c, off], recv_sem=ret_recv.at[c, ep],
-                device_id={"ep": owner}, device_id_type=MESH)
-            copy.start()
-            sends.append(copy)
-        returned[c, ep] = partial[c, ep]
-
-    for c in range(chunks):
-        for off in range(1, ep_count):
-            source = lax.rem(ep + off, ep_count)
-            pltpu.make_async_remote_copy(
-                src_ref=partial.at[c, source], dst_ref=returned.at[c, source],
-                send_sem=ret_send.at[c, off], recv_sem=ret_recv.at[c, source],
-                device_id={"ep": source}, device_id_type=MESH).wait_recv()
+        take_back(sibling, 0, cap, c, 0)
+        for off in range(1, pairs):
+            other = lax.rem(pair + pairs - off, pairs)
+            for who in (core, 1 - core):
+                for g, (low, high) in enumerate(row_groups):
+                    take_back(2 * other + who, low * piece, (high - low) * piece, c, g)
         for h in range(hid_count):
             block = returned[c, :, :, h * step:(h + 1) * step].reshape(ep_count * cap, step)
             owner_out[c, h] = jnp.dot(combine[...], block, preferred_element_type=F32).astype(BF16)
@@ -197,7 +234,7 @@
                 device_id={"hid": source}, device_id_type=MESH).wait_recv()
             total = total + owner_in[c, source].astype(F32)
         out[:, c * step:(c + 1) * step] = total.astype(BF16)
-    for copy in sends + forwards:
+    for copy in sends + list(forwards.values()):
         copy.wait_send()
 
 
@@ -226,7 +263,7 @@
             pltpu.VMEM((others, 2, cap, width // 2), BF16),
             pltpu.VMEM((cap, width), BF16),
             pltpu.VMEM((ep_count, cap, width), BF16),
-            pltpu.VMEM((ep_count * cap, inner), BF16),
+            pltpu.VMEM((ep_count, cap, inner), BF16),
             pltpu.VMEM((chunks, ep_count, cap, hid_count * step), BF16),
             pltpu.VMEM((chunks, ep_count, cap, hid_count * step), BF16),
             pltpu.VMEM((chunks, hid_count, rows, step), BF16),
@@ -236,8 +273,8 @@
             dma((ep_count, ROW_CHUNKS)),
             dma((ep_count // 2, ROW_CHUNKS, 2)),
             dma((ep_count // 2, ROW_CHUNKS, 2)),
-            dma((chunks, ep_count)),
-            dma((chunks, ep_count)),
+            dma((chunks, ep_count, 2)),
+            dma((chunks, ep_count, 2)),
             dma((chunks, hid_count)),
             dma((chunks, hid_count)),
         ],

time: 57.6 us -> 59.7 us (1.036)
  Pallas kernels: 55.7 us -> 57.9 us
    pallas_call x1, Pallas kernels: 55.7 us -> 57.9 us  [local(): pl.pallas_call(functools.partial(kernel, ep_count, hid_count), out_shape=...]
where the time goes in v3:
time: 59.7 us; the launch traced here: 59.6 us
  Pallas kernels  57.9 us (97%)
  local copies, waits for them, and re-layouts  1.67 us (3%)
    pallas_call x1, Pallas kernels, local(): pl.pallas_call(functools.partial(kernel, ep_count, hid_count), out_shape=...  57.9 us
    unnamed x1, local copies, waits for them, and re-layouts  1.67 us

profile of v3, /device:TPU:0, one launch (start us, length us, event | category | flops | bytes accessed | tf_op | source)
XLA Modules:
  0.0 59.6 jit_solution(13348160224365097433)
XLA Ops:
  0.0 57.9 %shard_map.64 = bf16[128,1024]{1,0:T(8,128)(2,1)} custom-call(bf16[128,4096]{1,0:T(8,128)(2,1)} %tokens.1, s32[2,128]{1,0:T(2,128)} %bitcast.2, f32[2,128]{1,0:T(2,128)} %bitcast.3, bf16[1,4096,384]{2,1,0:T(8,128)(2,1)} %w_gate.1, bf16[1,4096,384]{2,1,0:T(8,128)(2,1)} %w_up.1, bf16[1,384,4096]{2,1,0:T(8,128)(2,1)} %w_down.1), custom_call_target="tpu_custom_call" | custom-call | tf_op jit(solution)/shard_map/pallas_call | solution.py:252
  57.9 1.7 %copy.8 = bf16[128,1024]{1,0:T(8,128)(2,1)} copy(bf16[128,1024]{1,0:T(8,128)(2,1)} %shard_map.64) | data formatting | bytes 524288
